TPU v7x, 32 devices: a whole 2x2x4 slice. The times are simulated.
32 devices in a mesh: group: 4 (over z), member: 8 (over y, x, core).
Axes of the slice: x: 2, y: 2, z: 4, core: 2. Of those that a mesh axis runs over, the one named last changes fastest.
Arguments:
- hidden: bfloat16 [6144, 2048], P('group'), may hold values from -6 to 6
- token_slab: int32 [6144, 1], P(('group', 'member')), may hold values from 0 to 31; in each aligned block of 192 rows (0 to 191, 192 to 383, ...) at most 12 rows name the same one
- token_row: int32 [6144], P(('group', 'member')), may hold values from 0 to 8191
- slab_owner: int32 [32], replicated, may hold values from 0 to 31, each once
- ple_table: bfloat16 [262144, 256], P(('group', 'member')), may hold values from -0.375 to 0.375
- norm_gains: float32 [1, 3, 2048], replicated, may hold values from 0.1 to 1.9
- w_gate: bfloat16 [1, 2048, 8192], P(None, None, 'member'), may hold values from -0.125 to 0.125
- w_up: bfloat16 [1, 2048, 8192], P(None, None, 'member'), may hold values from -0.125 to 0.125
- w_down: bfloat16 [1, 8192, 2048], P(None, 'member'), may hold values from -0.0625 to 0.0625
- ple_gate: bfloat16 [1, 2048, 256], P(None, None, 'member'), may hold values from -0.125 to 0.125
- ple_proj: bfloat16 [1, 256, 2048], P(None, 'member'), may hold values from -0.375 to 0.375
Outputs:
- hidden_out: bfloat16 [6144, 2048], P('group')
Inputs may be any that keep to these rules, and one draw needn't show every extreme that they name: Within the 192 tokens of one device (aligned blocks of token_slab), no slab is named by more than 12 tokens. Each number appears once: slab s is stored in rows slab_owner[s] * 8192 to slab_owner[s] * 8192 + 8191 of ple_table.
All inputs are finite; a program needn't handle non-finite values.
Results may differ from a plain program's by a relative error of at most 0.0061.
Values may be sent and summed in bfloat16 or wider, within the bound.
No kernel may reach another device: no remote copies, remote signals or barrier semaphores. Data moves between devices by JAX's collectives and lax.ppermute only.
A program may use at most 128 MiB of HBM per device.

v0:
```python
import jax
import jax.numpy as jnp
from jax import lax
from jax.sharding import PartitionSpec as P

PLE = 256
epsilon = 1e-06


def norm_rows(values, scales):
    return values * lax.rsqrt(jnp.mean(values * values, axis=-1, keepdims=True) + epsilon) * scales


def lookup_rows(wanted, ple_table):
    flat_ids = wanted.reshape(-1) - 1
    one_hot = (
        flat_ids[:, None] == jnp.arange(ple_table.shape[0], dtype=jnp.int32)[None, :]
    ).astype(jnp.bfloat16)
    served = jnp.dot(one_hot, ple_table, preferred_element_type=jnp.float32).astype(jnp.bfloat16)
    return served.reshape(wanted.shape + (ple_table.shape[1],))


def request_slots(slab_ids, token_row, slab_owner, devices, slots):
    target = slab_owner[slab_ids]
    order = jnp.arange(token_row.shape[0], dtype=jnp.int32)
    earlier = (target[None, :] == target[:, None]) & (order[None, :] < order[:, None])
    slot_of = jnp.sum(earlier.astype(jnp.int32), axis=1)
    hit_map = (target[:, None, None] == jnp.arange(devices, dtype=jnp.int32)[None, :, None]) & (
        slot_of[:, None, None] == jnp.arange(slots, dtype=jnp.int32)[None, None, :]
    )
    requests = jnp.sum(jnp.where(hit_map, token_row[:, None, None] + 1, 0), axis=0)
    return (hit_map, requests)


def pick_rows(hit_map, returned):
    return jnp.einsum(
        "tdc,dcw->tw", hit_map.astype(jnp.bfloat16), returned, preferred_element_type=jnp.float32
    ).astype(jnp.bfloat16)


def combine_branch(current, partial_value, scales):
    share = lax.psum_scatter(partial_value, "member", scatter_dimension=1, tiled=True)
    share_width = share.shape[1]
    offset = lax.axis_index("member") * share_width
    squares = lax.psum(jnp.sum(share * share, axis=-1, keepdims=True), "member")
    normed = (
        share
        * lax.rsqrt(squares / (share_width * lax.axis_size("member")) + epsilon)
        * lax.dynamic_slice_in_dim(scales, offset, share_width, 0)
    )
    updated = lax.dynamic_slice_in_dim(current, offset, share_width, 1) + normed
    return lax.all_gather(updated, "member", axis=1, tiled=True)


def per_device(
    hidden,
    token_slab,
    token_row,
    slab_owner,
    ple_table,
    norm_gains,
    w_gate,
    w_up,
    w_down,
    ple_gate,
    ple_proj,
):
    members = lax.axis_size("member")
    devices = lax.axis_size("group") * members
    tokens_here = token_row.shape[0]
    slots = max(2, (2 * tokens_here + devices - 1) // devices)
    slab_ids = token_slab[:, 0]
    hit_map, requests = request_slots(slab_ids, token_row, slab_owner, devices, slots)
    grouped = requests.reshape(lax.axis_size("group"), members, slots)
    received = lax.all_to_all(
        lax.all_to_all(grouped, "group", split_axis=0, concat_axis=0, tiled=True),
        "member",
        split_axis=1,
        concat_axis=1,
        tiled=True,
    )
    served = lookup_rows(received, ple_table)
    returned = lax.all_to_all(
        lax.all_to_all(served, "group", split_axis=0, concat_axis=0, tiled=True),
        "member",
        split_axis=1,
        concat_axis=1,
        tiled=True,
    )
    own_rows = pick_rows(hit_map, returned.reshape(devices, slots, ple_table.shape[1]))
    per_member = ple_gate.shape[2]
    layers = w_gate.shape[0]
    pieces = own_rows.reshape(tokens_here, layers, members, per_member)
    columns = lax.all_to_all(pieces, "member", split_axis=2, concat_axis=0, tiled=True)
    ple_part = columns.reshape(-1, layers, per_member).astype(jnp.float32) * PLE**0.5
    current = hidden.astype(jnp.float32)
    normed = norm_rows(current, norm_gains[0, 0]).astype(jnp.bfloat16)
    gate_part = jnp.dot(normed, w_gate[0], preferred_element_type=jnp.float32)
    up_part = jnp.dot(normed, w_up[0], preferred_element_type=jnp.float32)
    activated = (jax.nn.gelu(gate_part, approximate=True) * up_part).astype(jnp.bfloat16)
    mlp_out = jnp.dot(activated, w_down[0], preferred_element_type=jnp.float32)
    current = combine_branch(current, mlp_out, norm_gains[0, 1])
    current_b = current.astype(jnp.bfloat16)
    ple_gate_out = jnp.dot(current_b, ple_gate[0], preferred_element_type=jnp.float32)
    ple_act = (jax.nn.gelu(ple_gate_out, approximate=True) * ple_part[:, 0, :]).astype(jnp.bfloat16)
    ple_out = jnp.dot(ple_act, ple_proj[0], preferred_element_type=jnp.float32)
    current = combine_branch(current, ple_out, norm_gains[0, 2])
    return current.astype(jnp.bfloat16)


def solution(mesh):
    return jax.shard_map(
        per_device,
        mesh=mesh,
        in_specs=(
            P("group", None),
            P(("group", "member"), None),
            P(("group", "member")),
            P(),
            P(("group", "member"), None),
            P(),
            P(None, None, "member"),
            P(None, None, "member"),
            P(None, "member", None),
            P(None, None, "member"),
            P(None, "member", None),
        ),
        out_specs=P("group", None),
        check_vma=False,
    )
```

profile of v0, /device:TPU:0, one launch (start us, length us, event | category | flops | bytes accessed | tf_op | source)
XLA Modules:
  0.0 417.3 jit_solution(211991118664863560)
XLA Ops:
  6.5 4.2 %multiply_reduce_fusion = f32[1536]{0:T(1024)S(1)} fusion(bf16[1536,2048]{1,0:T(8,128)(2,1)} %param.11), kind=kLoop, calls=%fused_computation.2 | loop fusion | flops 9435648 | bytes 6297600 | tf_op jit(solution)/shard_map/reduce_sum | solution.py:11
  10.8 0.4 copy-done.1
  11.2 10.4 %fusion.17 = f32[1536,1024]{1,0:T(8,128)} fusion(bf16[1,2048,1024]{2,1,0:T(8,128)(2,1)} %param.17, f32[2048]{0:T(1024)S(1)} %bitcast.75, f32[1536]{0:T(1024)S(1)} %add_rsqrt_fusion, bf16[1536,2048]{1,0:T(8,128)(2,1)S(1)} %copy-done.1), kind=kOutput, calls=%fused_computation.20 | convolution fusion | flops 6455033856 | bytes 16791552 | tf_op jit(solution)/shard_map/dot_general | solution.py:98
  21.6 22.6 %fusion.13 = f32[1536,2048]{1,0:T(8,128)} fusion(bf16[1,1024,2048]{2,1,0:T(8,128)(2,1)} %param.19, f32[1536,1024]{1,0:T(8,128)} %fusion.17, bf16[1,2048,1024]{2,1,0:T(8,128)(2,1)} %param.18, f32[2048]{0:T(1024)S(1)} %bitcast.76, f32[1536]{0:T(1024)S(1)} %add_rsqrt_fusion, bf16[1536,2048]{1,0:T(8,128)(2,1)} %param.11), kind=kOutput, calls=%fused_computation.17 | convolution fusion | flops 12913213440 | bytes 33568768 | tf_op jit(solution)/shard_map/dot_general | solution.py:101
  44.2 0.0 reduce-scatter.3.cloned.1.call-update
  44.2 0.2 all-gather.3.cloned.1.call-start
  44.5 9.5 %convert_element_type.38 = f32[1536,2048]{1,0:T(8,128)} convert(bf16[1536,2048]{1,0:T(8,128)(2,1)} %param.11) | non-fusion elementwise | flops 3145728 | bytes 18874368 | tf_op jit(solution)/shard_map/convert_element_type | solution.py:96
  54.0 85.1 %reduce-scatter.3.cloned.1.call-done = f32[1536,256]{1,0:T(8,128)} async-done(((f32[1536,2048]{1,0:T(8,128)}), f32[1536,256]{1,0:T(8,128)}) %reduce-scatter.3.cloned.1.call-update) | async-done | bytes 1572880 | tf_op jit(solution)/shard_map/reduce_scatter | solution.py:42
  139.1 1.7 multiply_reduce_fusion.2
  140.8 12.8 %psum.14 = f32[1536,1]{0,1:T(1,128)S(1)} all-reduce(f32[1536,1]{0,1:T(1,128)S(1)} %broadcast_in_dim.12), channel_id=1, replica_groups=mesh['group'=4,'member'=8] {'member'}, use_global_device_ids=true, to_apply=%region_3.4 | all-reduce | flops 1536 | bytes 12288 | tf_op jit(solution)/shard_map/psum | solution.py:45
  153.6 3.3 multiply_add_fusion.1
  156.9 0.0 all-gather.3.cloned.1.call-update
  156.9 0.0 reduce-scatter.5.cloned.1.call-start
  157.0 0.0 copy-done.2
  157.0 0.7 fusion.67
  157.7 0.7 fusion.66
  158.4 4.3 %compare_select_fusion.1 = (s32[192,1]{0,1:T(1,128)S(1)}, s32[192,1]{0,1:T(1,128)S(1)}) fusion(s32[]{:T(128)} %bitcast.31, s32[]{:T(128)} %bitcast.32, s32[]{:T(128)} %bitcast.33, s32[]{:T(128)} %bitcast.34, s32[]{:T(128)} %bitcast.35, s32[]{:T(128)} %bitcast.37, s32[]{:T(128)} %bitcast.36, s32[192,1]{0,1:T(1,128)S(1)} %copy-done.6), kind=kLoop, calls=%fused_computation.93 | loop fusion | flops 2880 | bytes 2332 | tf_op jit(solution)/shard_map/gather | solution.py:24
  162.7 0.1 compare_reduce_fusion.24
  162.8 15.6 %select_select_fusion = s32[192]{0:T(256)S(1)} fusion(pred[192]{0:T(512)(128)(4,1)S(1)} %get-tuple-element.29, pred[192]{0:T(512)(128)(4,1)S(1)} %get-tuple-element.28, pred[192]{0:T(512)(128)(4,1)S(1)} %get-tuple-element.27, pred[192]{0:T(512)(128)(4,1)S(1)} %get-tuple-element.26, pred[192]{0:T(512)(128)(4,1)S(1)} %get-tuple-element.25, ...), kind=kLoop, calls=%fused_computation.99 | loop fusion | flops 4800 | bytes 6436 | tf_op jit(solution)/shard_map/gather | solution.py:24
  178.4 0.2 convert_reduce_fusion
  178.6 0.0 copy-done.5
  178.7 0.3 fusion.26
  179.0 0.1 copy.42
  179.1 10.0 %all_to_all.29 = s32[4,8,12]{2,1,0:T(8,128)S(1)} all-to-all(s32[4,8,12]{2,1,0:T(8,128)S(1)} %bitcast.74), channel_id=1, replica_groups=mesh['group'=4,'member'=8] {'group'}, dimensions={0} | all-to-all | bytes 3072 | tf_op jit(solution)/shard_map/all_to_all | solution.py:76
  189.0 7.6 %all_to_all.30 = s32[4,8,12]{2,0,1:T(4,128)S(1)} all-to-all(s32[4,8,12]{2,0,1:T(4,128)S(1)} %copy.43), channel_id=1, replica_groups=mesh['group'=4,'member'=8] {'member'}, dimensions={1} | all-to-all | bytes 3072 | tf_op jit(solution)/shard_map/all_to_all | solution.py:75
  196.7 0.1 sub.7
  196.8 0.0 copy-start.3
  196.8 4.6 %fusion.23 = bf16[384,256]{1,0:T(8,128)(2,1)S(1)} fusion(bf16[8192,256]{1,0:T(8,128)(2,1)} %param.15, s32[384]{0:T(512)S(1)} %sub.7), kind=kOutput, calls=%fused_computation.30 | convolution fusion | flops 1613856768 | bytes 4392448 | tf_op jit(solution)/shard_map/dot_general | solution.py:19
  201.4 0.1 copy.45
  201.5 10.0 %all_to_all.31 = bf16[4,8,12,256]{3,1,2,0:T(8,128)(2,1)S(1)} all-to-all(bf16[4,8,12,256]{3,1,2,0:T(8,128)(2,1)S(1)} %copy.45), channel_id=1, replica_groups=mesh['group'=4,'member'=8] {'group'}, dimensions={0} | all-to-all | bytes 393216 | tf_op jit(solution)/shard_map/all_to_all | solution.py:84
  211.5 0.2 copy.46
  211.7 11.1 %all_to_all.32 = bf16[4,8,12,256]{3,0,2,1:T(4,128)(2,1)S(1)} all-to-all(bf16[4,8,12,256]{3,0,2,1:T(4,128)(2,1)S(1)} %copy.46), channel_id=1, replica_groups=mesh['group'=4,'member'=8] {'member'}, dimensions={1} | all-to-all | bytes 393216 | tf_op jit(solution)/shard_map/all_to_all | solution.py:83
  222.8 0.3 fusion.24
  223.1 0.1 copy.48
  223.2 8.2 %all_to_all.33 = bf16[192,1,8,32]{0,3,1,2:T(8,128)(2,1)S(1)} all-to-all(bf16[192,1,8,32]{0,3,1,2:T(8,128)(2,1)S(1)} %bitcast.73), channel_id=1, replica_groups=mesh['group'=4,'member'=8] {'member'}, dimensions={2} | all-to-all | bytes 196608 | tf_op jit(solution)/shard_map/all_to_all | solution.py:94
  231.4 0.2 copy.50
  231.5 0.1 mul.170
  231.7 2.3 all-gather.3.cloned.1.call-done
  234.0 12.7 %fusion.43 = f32[1536,2048]{1,0:T(8,128)} fusion(f32[1536,32]{0,1:T(8,128)S(1)} %mul.170, f32[1536,2048]{1,0:T(8,128)} %all-gather.3.cloned.1.call-done, bf16[1,32,2048]{2,1,0:T(8,128)(2,1)S(1)} %copy-done, bf16[1,2048,32]{1,2,0:T(8,128)(2,1)S(1)} %copy-done.3), kind=kOutput, calls=%fused_computation.47 | convolution fusion | flops 406290432 | bytes 25624576 | tf_op jit(solution)/shard_map/dot_general | solution.py:106
  246.7 0.0 reduce-scatter.5.cloned.1.call-update
  246.7 0.0 all-gather.5.cloned.1.call-start
  246.8 93.1 %reduce-scatter.5.cloned.1.call-done = f32[1536,256]{1,0:T(8,128)} async-done(((f32[1536,2048]{1,0:T(8,128)}), f32[1536,256]{1,0:T(8,128)}) %reduce-scatter.5.cloned.1.call-update) | async-done | bytes 1572880 | tf_op jit(solution)/shard_map/reduce_scatter | solution.py:42
  339.8 1.7 multiply_reduce_fusion.1
  341.5 12.8 %psum.15 = f32[1536,1]{0,1:T(1,128)S(1)} all-reduce(f32[1536,1]{0,1:T(1,128)S(1)} %broadcast_in_dim.19), channel_id=1, replica_groups=mesh['group'=4,'member'=8] {'member'}, use_global_device_ids=true, to_apply=%region_8.9 | all-reduce | flops 1536 | bytes 12288 | tf_op jit(solution)/shard_map/psum | solution.py:45
  354.4 3.0 multiply_add_fusion
  357.4 0.0 all-gather.5.cloned.1.call-update
  357.4 46.7 %all-gather.5.cloned.1.call-done = bf16[1536,2048]{1,0:T(8,128)(2,1)} async-done(((bf16[1536,256]{1,0:T(8,128)(2,1)}), bf16[1536,2048]{1,0:T(8,128)(2,1)}) %all-gather.5.cloned.1.call-update) | async-done | bytes 6291472 | tf_op jit(solution)/shard_map/all_gather | solution.py:52
  404.1 6.6 %copy.57 = bf16[1536,2048]{1,0:T(8,128)(2,1)} copy(bf16[1536,2048]{1,0:T(8,128)(2,1)} %all-gather.5.cloned.1.call-done) | data formatting | bytes 12582912
  (26 shorter events, 0.2 us)
Async XLA Ops:
  6.5 227.5 %copy-start = (bf16[1,32,2048]{2,1,0:T(8,128)(2,1)S(1)}, bf16[1,32,2048]{2,1,0:T(8,128)(2,1)}, u32[]{:S(2)}) copy-start(bf16[1,32,2048]{2,1,0:T(8,128)(2,1)} %param.21) | copy-start | bytes 393220
  6.5 4.3 %copy-start.4 = (f32[1,3,2048]{2,0,1:T(1,128)S(1)}, f32[1,3,2048]{2,0,1:T(1,128)}, u32[]{:S(2)}) copy-start(f32[1,3,2048]{2,0,1:T(1,128)} %param.16) | copy-start | bytes 73732
  6.5 132.5 %reduce-scatter.3.cloned.1.call-start = ((), (), s32[]{:S(2)}) async-start(), calls=%async_computation.7 | async-start | bytes 14155776 | tf_op jit(solution)/shard_map/reduce_scatter | solution.py:42
  6.5 4.6 %copy-start.1 = (bf16[1536,2048]{1,0:T(8,128)(2,1)S(1)}, bf16[1536,2048]{1,0:T(8,128)(2,1)}, u32[]{:S(2)}) copy-start(bf16[1536,2048]{1,0:T(8,128)(2,1)} %param.11) | copy-start | bytes 18874372
  44.2 189.8 %all-gather.3.cloned.1.call-start = ((), (), s32[]{:S(2)}) async-start(), calls=%async_computation.8 | async-start | bytes 14155776 | tf_op jit(solution)/shard_map/all_gather | solution.py:52
  54.0 103.0 %copy-start.2 = (s32[32]{0:T(128)S(1)}, s32[32]{0:T(128)}, u32[]{:S(2)}) copy-start(s32[32]{0:T(128)} %param.14) | copy-start | bytes 388
  54.0 104.4 %copy-start.6 = (s32[192,1]{0,1:T(1,128)S(1)}, s32[192,1]{0,1:T(1,128)}, u32[]{:S(2)}) copy-start(s32[192,1]{0,1:T(1,128)} %param.12) | copy-start | bytes 2308
  54.0 124.6 %copy-start.5 = (s32[192]{0:T(256)S(1)}, s32[192]{0:T(256)}, u32[]{:S(2)}) copy-start(s32[192]{0:T(256)} %param.13) | copy-start | bytes 2308
  156.9 182.9 %reduce-scatter.5.cloned.1.call-start = ((), (), s32[]{:S(2)}) async-start(), calls=%async_computation.9 | async-start | bytes 14155776 | tf_op jit(solution)/shard_map/reduce_scatter | solution.py:42
  196.8 37.2 %copy-start.3 = (bf16[1,2048,32]{1,2,0:T(8,128)(2,1)S(1)}, bf16[1,2048,32]{1,2,0:T(8,128)(2,1)}, u32[]{:S(2)}) copy-start(bf16[1,2048,32]{1,2,0:T(8,128)(2,1)} %param.20) | copy-start | bytes 393220
  246.7 157.4 %all-gather.5.cloned.1.call-start = ((), (), s32[]{:S(2)}) async-start(), calls=%async_computation.10 | async-start | bytes 7077888 | tf_op jit(solution)/shard_map/all_gather | solution.py:52
Sparse Core Ops, SparseCore 0:
  44.4 94.6 reduce-scatter.2
  157.0 76.9 all-gather.2
  246.8 92.9 reduce-scatter.4
  357.5 46.5 all-gather.4
where the time goes:
time: 418 us; the launch traced here: 417 us
  waiting for transfers between devices  227 us (54%)
  blocking collectives  72.4 us (17%)
  matrix products  50.5 us (12%)
  other arithmetic  44 us (11%)
  between operations  13.4 us (3%)
  local copies, waits for them, and re-layouts  9.3 us (2%)
    reduce_scatter x2, waiting for transfers between devices, combine_branch(): lax.psum_scatter(partial_value, 'member', scatter_dimension=1, tiled=True)  178 us
    all_gather x2, waiting for transfers between devices, combine_branch(): return lax.all_gather(updated, 'member', axis=1, tiled=True)  49.1 us
    psum x2, blocking collectives, combine_branch(): squares = lax.psum(jnp.sum(share * share, axis=-1, keepdims=True), 'member')  25.5 us
    dot_general x1, matrix products, per_device(): mlp_out = jnp.dot(activated, w_down[0], preferred_element_type=jnp.float32)  22.6 us
    gather x3, other arithmetic, request_slots(): target = slab_owner[slab_ids]  20 us
    dot_general x1, matrix products, per_device(): ple_out = jnp.dot(ple_act, ple_proj[0], preferred_element_type=jnp.float32)  12.7 us
    all_to_all x1, blocking collectives, per_device(): lax.all_to_all(lax.all_to_all(served, 'group', split_axis=0, concat_axis=...  11.1 us
    dot_general x1, matrix products, per_device(): gate_part = jnp.dot(normed, w_gate[0], preferred_element_type=jnp.float32)  10.4 us
  transfers between devices with their start and end apart: 4, of which 4 were waited for; matrix products, arithmetic and copies ran while one was open for 9% of the time, Pallas kernels for 0%

commit v1 on v0

--- a/solution.py
+++ b/solution.py
@@ -5,6 +5,11 @@
 
 PLE = 256
 epsilon = 1e-06
+
+
+def exchange_gather(array, axis, d):
+    sent = jnp.stack([array] * lax.axis_size(axis))
+    return jnp.concatenate(lax.all_to_all(sent, axis, 0, 0), axis=d)
 
 
 def norm_rows(values, scales):
@@ -49,7 +54,7 @@
         * lax.dynamic_slice_in_dim(scales, offset, share_width, 0)
     )
     updated = lax.dynamic_slice_in_dim(current, offset, share_width, 1) + normed
-    return lax.all_gather(updated, "member", axis=1, tiled=True)
+    return exchange_gather(updated, "member", 1)
 
 
 def per_device(

time: 418 us -> 537 us (1.28)
  blocking collectives: 72.4 us -> 131 us
  local copies, waits for them, and re-layouts: 9.3 us -> 53 us
  starting transfers between devices: 0.31 us -> 13 us
  waiting for transfers between devices: 227 us -> 236 us
    all_to_all x0 -> x3, waiting for transfers between devices: none -> 139 us  [the longest x1 139 us: exchange_gather(): return jnp.concatenate(lax.all_to_all(sent, axis, 0, 0), axis=d)]
    reduce_scatter x2, waiting for transfers between devices: 178 us -> 97.5 us  [combine_branch(): lax.psum_scatter(partial_value, 'member', scatter_dimension=1, tiled=True)]
    all_to_all x2 -> x1, blocking collectives: 19.3 us -> 74.9 us  [exchange_gather(): return jnp.concatenate(lax.all_to_all(sent, axis, 0, 0), axis=d)]
    all_gather x2 -> x0, waiting for transfers between devices: 49.1 us -> none  [combine_branch(): return lax.all_gather(updated, 'member', axis=1, tiled=True)]
    all_to_all x0 -> x2, local copies, waits for them, and re-layouts: none -> 18.6 us  [exchange_gather(): return jnp.concatenate(lax.all_to_all(sent, axis, 0, 0), axis=d)]
    reshape x0 -> x1, local copies, waits for them, and re-layouts: none -> 15.2 us  [exchange_gather(): return jnp.concatenate(lax.all_to_all(sent, axis, 0, 0), axis=d)]
    all_to_all x0 -> x3, starting transfers between devices: none -> 13 us  [the longest x1 5.34 us: exchange_gather(): return jnp.concatenate(lax.all_to_all(sent, axis, 0, 0), axis=d)]
    convert_element_type x0 -> x1, local copies, waits for them, and re-layouts: none -> 8.61 us  [per_device(): return current.astype(jnp.bfloat16)]
  transfers between devices with their start and end apart: 4 -> 5, of which waited for: 4 -> 3; matrix products, arithmetic and copies ran while one was open for 9% -> 11% of each run, Pallas kernels for 0% -> 0%
where the time goes in v1:
time: 537 us; the launch traced here: 536 us
  waiting for transfers between devices  236 us (44%)
  blocking collectives  131 us (24%)
  local copies, waits for them, and re-layouts  53 us (10%)
  matrix products  48 us (9%)
  other arithmetic  41.4 us (8%)
  between operations  13.7 us (3%)
  starting transfers between devices  13 us (2%)
    all_to_all x1, waiting for transfers between devices, exchange_gather(): return jnp.concatenate(lax.all_to_all(sent, axis, 0, 0), axis=d)  139 us
    reduce_scatter x2, waiting for transfers between devices, combine_branch(): lax.psum_scatter(partial_value, 'member', scatter_dimension=1, tiled=True)  97.5 us
    all_to_all x1, blocking collectives, exchange_gather(): return jnp.concatenate(lax.all_to_all(sent, axis, 0, 0), axis=d)  74.9 us
    psum x2, blocking collectives, combine_branch(): squares = lax.psum(jnp.sum(share * share, axis=-1, keepdims=True), 'member')  25.5 us
    dot_general x1, matrix products, per_device(): mlp_out = jnp.dot(activated, w_down[0], preferred_element_type=jnp.float32)  22.6 us
    gather x3, other arithmetic, request_slots(): target = slab_owner[slab_ids]  20.1 us
    all_to_all x2, local copies, waits for them, and re-layouts, exchange_gather(): return jnp.concatenate(lax.all_to_all(sent, axis, 0, 0), axis=d)  18.6 us
    reshape x1, local copies, waits for them, and re-layouts, exchange_gather(): return jnp.concatenate(lax.all_to_all(sent, axis, 0, 0), axis=d)  15.2 us
  transfers between devices with their start and end apart: 5, of which 3 were waited for; matrix products, arithmetic and copies ran while one was open for 11% of the time, Pallas kernels for 0%

profile of v1, /device:TPU:0, one launch (start us, length us, event | category | flops | bytes accessed | tf_op | source)
XLA Modules:
  0.0 535.8 jit_solution(17045676051018718924)
XLA Ops:
  6.5 4.2 multiply_reduce_fusion
  10.8 0.4 copy-done.1
  11.2 10.4 %fusion.15 = f32[1536,1024]{1,0:T(8,128)} fusion(bf16[1,2048,1024]{2,1,0:T(8,128)(2,1)} %param.17, f32[2048]{0:T(1024)S(1)} %bitcast.91, f32[1536]{0:T(1024)S(1)} %add_rsqrt_fusion, bf16[1536,2048]{1,0:T(8,128)(2,1)S(1)} %copy-done.1), kind=kOutput, calls=%fused_computation.19 | convolution fusion | flops 6455033856 | bytes 16791552 | tf_op jit(solution)/shard_map/dot_general | solution.py:103
  21.6 22.6 %fusion.11 = f32[1536,2048]{1,0:T(8,128)} fusion(bf16[1,1024,2048]{2,1,0:T(8,128)(2,1)} %param.19, f32[1536,1024]{1,0:T(8,128)} %fusion.15, bf16[1,2048,1024]{2,1,0:T(8,128)(2,1)} %param.18, f32[2048]{0:T(1024)S(1)} %bitcast.92, f32[1536]{0:T(1024)S(1)} %add_rsqrt_fusion, bf16[1536,2048]{1,0:T(8,128)(2,1)} %param.11), kind=kOutput, calls=%fused_computation.16 | convolution fusion | flops 12913213440 | bytes 33568768 | tf_op jit(solution)/shard_map/dot_general | solution.py:106
  44.2 0.0 reduce-scatter.3.cloned.1.call-update
  44.2 0.6 copy-done.2
  44.9 0.7 fusion.61
  45.6 0.7 fusion.60
  46.3 4.3 compare_select_fusion.1
  50.7 0.1 compare_reduce_fusion.24
  50.7 15.6 %select_select_fusion = s32[192]{0:T(256)S(1)} fusion(pred[192]{0:T(512)(128)(4,1)S(1)} %get-tuple-element.29, pred[192]{0:T(512)(128)(4,1)S(1)} %get-tuple-element.28, pred[192]{0:T(512)(128)(4,1)S(1)} %get-tuple-element.27, pred[192]{0:T(512)(128)(4,1)S(1)} %get-tuple-element.26, pred[192]{0:T(512)(128)(4,1)S(1)} %get-tuple-element.25, ...), kind=kLoop, calls=%fused_computation.99 | loop fusion | flops 4800 | bytes 6436 | tf_op jit(solution)/shard_map/gather | solution.py:29
  66.4 0.2 convert_reduce_fusion
  66.6 0.3 fusion.24
  66.9 0.1 copy.53
  67.0 11.7 %all_to_all.39 = s32[4,8,12]{2,1,0:T(8,128)S(1)} all-to-all(s32[4,8,12]{2,1,0:T(8,128)S(1)} %bitcast.90), channel_id=1, replica_groups=mesh['group'=4,'member'=8] {'group'}, dimensions={0} | all-to-all | bytes 3072 | tf_op jit(solution)/shard_map/all_to_all | solution.py:81
  78.8 8.6 %all_to_all.40 = s32[4,8,12]{2,0,1:T(4,128)S(1)} all-to-all(s32[4,8,12]{2,0,1:T(4,128)S(1)} %copy.54), channel_id=1, replica_groups=mesh['group'=4,'member'=8] {'member'}, dimensions={1} | all-to-all | bytes 3072 | tf_op jit(solution)/shard_map/all_to_all | solution.py:80
  87.3 0.1 sub.7
  87.4 4.7 fusion.21
  92.2 0.1 copy.56
  92.3 9.8 %all_to_all.41 = bf16[4,8,12,256]{3,1,2,0:T(8,128)(2,1)S(1)} all-to-all(bf16[4,8,12,256]{3,1,2,0:T(8,128)(2,1)S(1)} %copy.56), channel_id=1, replica_groups=mesh['group'=4,'member'=8] {'group'}, dimensions={0} | all-to-all | bytes 393216 | tf_op jit(solution)/shard_map/all_to_all | solution.py:89
  102.1 0.8 copy.57
  103.0 3.4 all-to-all-start.4
  106.4 8.8 %convert_element_type.47 = f32[1536,2048]{1,0:T(8,128)} convert(bf16[1536,2048]{1,0:T(8,128)(2,1)} %param.11) | non-fusion elementwise | flops 3145728 | bytes 18874368 | tf_op jit(solution)/shard_map/convert_element_type | solution.py:101
  115.1 0.3 fusion.22
  115.4 0.8 copy.59
  116.2 4.3 all-to-all-start.5
  120.4 22.3 %reduce-scatter.3.cloned.1.call-done = f32[1536,256]{1,0:T(8,128)} async-done(((f32[1536,2048]{1,0:T(8,128)}), f32[1536,256]{1,0:T(8,128)}) %reduce-scatter.3.cloned.1.call-update) | async-done | bytes 1572880 | tf_op jit(solution)/shard_map/reduce_scatter | solution.py:47
  142.8 1.7 multiply_reduce_fusion.2
  144.5 12.8 %psum.14 = f32[1536,1]{0,1:T(1,128)S(1)} all-reduce(f32[1536,1]{0,1:T(1,128)S(1)} %broadcast_in_dim.12), channel_id=1, replica_groups=mesh['group'=4,'member'=8] {'member'}, use_global_device_ids=true, to_apply=%region_3.4 | all-reduce | flops 1536 | bytes 12288 | tf_op jit(solution)/shard_map/psum | solution.py:50
  157.3 2.2 multiply_add_fusion.1
  159.4 5.6 %stack.4 = f32[8,1536,256]{2,1,0:T(8,128)} broadcast(f32[1536,256]{1,0:T(8,128)S(1)} %multiply_add_fusion.1), dimensions={1,2} | broadcast | bytes 14155776 | tf_op jit(solution)/shard_map/stack | solution.py:11
  165.0 5.3 all-to-all-start
  170.3 0.0 reduce-scatter.5.cloned.1.call-start
  170.4 0.2 copy.61
  170.6 0.1 mul.170
  170.7 138.6 %all-to-all-done = f32[8,1536,256]{2,1,0:T(8,128)} async-done(((f32[8,1536,256]{2,1,0:T(8,128)}), f32[8,1536,256]{2,1,0:T(8,128)}, u32[]{:S(2)}, u32[]{:S(2)}) %all-to-all-start) | async-done | bytes 12582944 | tf_op jit(solution)/shard_map/all_to_all | solution.py:12
  309.3 10.0 %copy.51 = bf16[8,1536,256]{1,2,0:T(8,128)(2,1)} copy(f32[8,1536,256]{2,1,0:T(8,128)} %all-to-all-done) | data formatting | bytes 18874368 | tf_op jit(solution)/shard_map/all_to_all | solution.py:12
  319.3 10.1 %fusion.39 = f32[1536,2048]{1,0:T(8,128)} fusion(bf16[1,32,2048]{2,1,0:T(8,128)(2,1)S(1)} %copy-done, f32[1536,32]{0,1:T(8,128)S(1)} %mul.170, bf16[1536,2048]{0,1:T(8,128)(2,1)} %bitcast.88, bf16[1,2048,32]{1,2,0:T(8,128)(2,1)S(1)} %copy-done.3), kind=kOutput, calls=%fused_computation.53 | convolution fusion | flops 403144704 | bytes 19333120 | tf_op jit(solution)/shard_map/dot_general | solution.py:111
  329.4 0.0 reduce-scatter.5.cloned.1.call-update
  329.4 15.2 %copy.65 = f32[8,192,8,256]{3,2,0,1:T(8,128)} copy(f32[8,192,8,256]{3,2,1,0:T(8,128)} %bitcast.56) | data formatting | bytes 25165824 | tf_op jit(solution)/shard_map/reshape | solution.py:12
  344.6 75.1 %reduce-scatter.5.cloned.1.call-done = f32[1536,256]{1,0:T(8,128)} async-done(((f32[1536,2048]{1,0:T(8,128)}), f32[1536,256]{1,0:T(8,128)}) %reduce-scatter.5.cloned.1.call-update) | async-done | bytes 1572880 | tf_op jit(solution)/shard_map/reduce_scatter | solution.py:47
  419.8 1.7 multiply_reduce_fusion.1
  421.5 12.8 %psum.15 = f32[1536,1]{0,1:T(1,128)S(1)} all-reduce(f32[1536,1]{0,1:T(1,128)S(1)} %broadcast_in_dim.19), channel_id=1, replica_groups=mesh['group'=4,'member'=8] {'member'}, use_global_device_ids=true, to_apply=%region_8.9 | all-reduce | flops 1536 | bytes 12288 | tf_op jit(solution)/shard_map/psum | solution.py:50
  434.3 2.2 multiply_add_fusion
  436.4 0.4 stack.5
  436.9 74.9 %all_to_all.42 = bf16[8,1536,256]{2,1,0:T(8,128)(2,1)} all-to-all(bf16[8,1536,256]{2,1,0:T(8,128)(2,1)S(1)} %stack.5), channel_id=1, replica_groups=mesh['group'=4,'member'=8] {'member'}, dimensions={0} | all-to-all | bytes 12582912 | tf_op jit(solution)/shard_map/all_to_all | solution.py:12
  511.7 8.6 %copy.62 = bf16[8,1536,256]{1,2,0:T(8,128)(2,1)} copy(bf16[8,1536,256]{2,1,0:T(8,128)(2,1)} %all_to_all.42) | data formatting | bytes 12582912 | tf_op jit(solution)/shard_map/all_to_all | solution.py:12
  520.3 8.6 %copy.63 = bf16[1536,2048]{1,0:T(8,128)(2,1)} copy(bf16[1536,2048]{0,1:T(8,128)(2,1)} %bitcast.87) | data formatting | bytes 12582912 | tf_op jit(solution)/shard_map/convert_element_type | solution.py:113
  (30 shorter events, 0.2 us)
Async XLA Ops:
  6.5 312.8 %copy-start = (bf16[1,32,2048]{2,1,0:T(8,128)(2,1)S(1)}, bf16[1,32,2048]{2,1,0:T(8,128)(2,1)}, u32[]{:S(2)}) copy-start(bf16[1,32,2048]{2,1,0:T(8,128)(2,1)} %param.21) | copy-start | bytes 393220
  6.5 4.3 copy-start.4
  6.5 136.2 %reduce-scatter.3.cloned.1.call-start = ((), (), s32[]{:S(2)}) async-start(), calls=%async_computation.9 | async-start | bytes 14155776 | tf_op jit(solution)/shard_map/reduce_scatter | solution.py:47
  6.5 4.6 copy-start.1
  44.2 0.7 copy-start.2
  44.2 2.1 copy-start.6
  44.2 22.4 %copy-start.5 = (s32[192]{0:T(256)S(1)}, s32[192]{0:T(256)}, u32[]{:S(2)}) copy-start(s32[192]{0:T(256)} %param.13) | copy-start | bytes 2308
  103.0 12.2 %all-to-all-start.4 = ((bf16[4,8,12,256]{3,0,2,1:T(4,128)(2,1)}), bf16[4,8,12,256]{3,0,2,1:T(4,128)(2,1)S(1)}, u32[]{:S(2)}, u32[]{:S(2)}) async-start(bf16[4,8,12,256]{3,0,2,1:T(4,128)(2,1)} %copy.57), calls=%async_computation.5 | async-start | bytes 393216 | tf_op jit(solution)/shard_map/all_to_all | solution.py:88
  116.2 43.3 %all-to-all-start.5 = ((bf16[192,1,8,32]{0,3,1,2:T(8,128)(2,1)}), bf16[192,1,8,32]{0,3,1,2:T(8,128)(2,1)S(1)}, u32[]{:S(2)}, u32[]{:S(2)}) async-start(bf16[192,1,8,32]{0,3,1,2:T(8,128)(2,1)} %bitcast.46), calls=%async_computation.6 | async-start | bytes 262144 | tf_op jit(solution)/shard_map/all_to_all | solution.py:99
  165.0 144.3 %all-to-all-start = ((f32[8,1536,256]{2,1,0:T(8,128)}), f32[8,1536,256]{2,1,0:T(8,128)}, u32[]{:S(2)}, u32[]{:S(2)}) async-start(f32[8,1536,256]{2,1,0:T(8,128)} %stack.4), calls=%async_computation.1 | async-start | bytes 25165824 | tf_op jit(solution)/shard_map/all_to_all | solution.py:12
  170.3 249.4 %reduce-scatter.5.cloned.1.call-start = ((), (), s32[]{:S(2)}) async-start(), calls=%async_computation.10 | async-start | bytes 14155776 | tf_op jit(solution)/shard_map/reduce_scatter | solution.py:47
  170.7 148.6 %copy-start.3 = (bf16[1,2048,32]{1,2,0:T(8,128)(2,1)S(1)}, bf16[1,2048,32]{1,2,0:T(8,128)(2,1)}, u32[]{:S(2)}) copy-start(bf16[1,2048,32]{1,2,0:T(8,128)(2,1)} %param.20) | copy-start | bytes 393220
Sparse Core Ops, SparseCore 0:
  44.4 98.3 reduce-scatter.2
  329.5 90.2 reduce-scatter.4
